TPU v7x, 32 devices: a whole 2x2x4 slice. The times are simulated.
32 devices in a mesh: plane: 4 (over y, x), tile: 8 (over z, core).
Axes of the slice: x: 2, y: 2, z: 4, core: 2. Of those that a mesh axis runs over, the one named last changes fastest.
Arguments:
- visibility: float32 [2, 65536], P(None, ('plane', 'tile')), may hold values from -6 to 6
- target: int32 [65536, 1], P(('plane', 'tile')), may hold values from 0 to 31; in each aligned block of 2048 rows (0 to 2047, 2048 to 4095, ...) at most 128 rows name the same one
- offset: int32 [65536], P(('plane', 'tile')), may hold values from 0 to 2097151
- taps: float32 [8], replicated, may hold values from 0.1 to 1
- w_plane: float32 [4], P('plane'), may hold values from -300 to 300
Outputs:
- dirty_image: float32 [4096, 4096], P('plane', 'tile')
Inputs may be any that keep to these rules, and one draw needn't show every extreme that they name: `target`: among the rows of one device no value occurs more than 128 times, and some value occurs exactly 128 times.
All inputs are finite; a program needn't handle non-finite values.
Results may differ from a plain program's by a relative error of at most 0.0042.
Values sent between devices are 32-bit elements; how exact they have to be, the bound alone decides.
A program may use at most 128 MiB of HBM per device.

v0:
```python
import math
import jax
import jax.numpy as jnp
from jax import lax
from jax.sharding import PartitionSpec as P

G = 4096
HIGHEST = lax.Precision.HIGHEST


def shifted(x, axis, by):
    length = lax.axis_size(axis)
    return lax.ppermute(x, axis, [(i, (i + by) % length) for i in range(length)])


def direction(index, length):
    return ((index + length // 2) % length - length // 2).astype(jnp.float32) * (0.5 / length)


def angle_table(first, second, length):
    product = (
        jnp.arange(first, dtype=jnp.int32)[:, None]
        * jnp.arange(second, dtype=jnp.int32)[None, :]
        % length
    )
    angles = product.astype(jnp.float32) * (2.0 * math.pi / length)
    return (jnp.cos(angles), jnp.sin(angles))


def split_length(length):
    inner_len = math.gcd(length, 128)
    return (length // inner_len, inner_len)


def transform_last(real_part, imag_part):
    length = real_part.shape[-1]
    outer_len, inner_len = split_length(length)
    real_grid = real_part.reshape(-1, outer_len, inner_len)
    imag_grid = imag_part.reshape(-1, outer_len, inner_len)
    cos_one, sin_one = angle_table(outer_len, outer_len, outer_len)
    first_re = jnp.einsum("rab,ak->rkb", real_grid, cos_one, precision=HIGHEST) - jnp.einsum(
        "rab,ak->rkb", imag_grid, sin_one, precision=HIGHEST
    )
    first_im = jnp.einsum("rab,ak->rkb", real_grid, sin_one, precision=HIGHEST) + jnp.einsum(
        "rab,ak->rkb", imag_grid, cos_one, precision=HIGHEST
    )
    cos_tw, sin_tw = angle_table(outer_len, inner_len, length)
    twist_re = first_re * cos_tw - first_im * sin_tw
    twist_im = first_re * sin_tw + first_im * cos_tw
    cos_two, sin_two = angle_table(inner_len, inner_len, inner_len)
    out_re = jnp.einsum("rkb,bq->rqk", twist_re, cos_two, precision=HIGHEST) - jnp.einsum(
        "rkb,bq->rqk", twist_im, sin_two, precision=HIGHEST
    )
    out_im = jnp.einsum("rkb,bq->rqk", twist_re, sin_two, precision=HIGHEST) + jnp.einsum(
        "rkb,bq->rqk", twist_im, cos_two, precision=HIGHEST
    )
    return (out_re.reshape(-1, length), out_im.reshape(-1, length))


def transform_first(real_part, imag_part):
    length = real_part.shape[0]
    outer_len, inner_len = split_length(length)
    real_grid = real_part.reshape(outer_len, inner_len, -1)
    imag_grid = imag_part.reshape(outer_len, inner_len, -1)
    cos_one, sin_one = angle_table(outer_len, outer_len, outer_len)
    first_re = jnp.einsum("abc,ak->kbc", real_grid, cos_one, precision=HIGHEST) - jnp.einsum(
        "abc,ak->kbc", imag_grid, sin_one, precision=HIGHEST
    )
    first_im = jnp.einsum("abc,ak->kbc", real_grid, sin_one, precision=HIGHEST) + jnp.einsum(
        "abc,ak->kbc", imag_grid, cos_one, precision=HIGHEST
    )
    cos_tw, sin_tw = angle_table(outer_len, inner_len, length)
    twist_re = first_re * cos_tw[:, :, None] - first_im * sin_tw[:, :, None]
    twist_im = first_re * sin_tw[:, :, None] + first_im * cos_tw[:, :, None]
    cos_two, sin_two = angle_table(inner_len, inner_len, inner_len)
    out_re = jnp.einsum("kbc,bq->qkc", twist_re, cos_two, precision=HIGHEST) - jnp.einsum(
        "kbc,bq->qkc", twist_im, sin_two, precision=HIGHEST
    )
    out_im = jnp.einsum("kbc,bq->qkc", twist_re, sin_two, precision=HIGHEST) + jnp.einsum(
        "kbc,bq->qkc", twist_im, cos_two, precision=HIGHEST
    )
    return (out_re.reshape(length, -1), out_im.reshape(length, -1))


def grid_block(received, taps, start, block_len, band_rows, totals):
    piece = lax.dynamic_slice_in_dim(received, start, block_len, 1)
    encoded = jnp.maximum(piece[2].astype(jnp.int32) - 1, 0)
    band_row = encoded // G
    column = encoded % G
    kernel_len = taps.shape[0]
    taps_low = taps.astype(jnp.bfloat16)
    weight_re = (taps[None, :] * piece[0][:, None]).astype(jnp.bfloat16)
    weight_im = (taps[None, :] * piece[1][:, None]).astype(jnp.bfloat16)
    rel_row = jnp.arange(band_rows, dtype=jnp.int32)[None, :] - band_row[:, None]
    rel_col = (jnp.arange(G, dtype=jnp.int32)[None, :] - column[:, None]) % G
    row_re = jnp.zeros((block_len, band_rows), jnp.bfloat16)
    row_im = jnp.zeros((block_len, band_rows), jnp.bfloat16)
    col_table = jnp.zeros((block_len, G), jnp.bfloat16)
    for tap_index in range(kernel_len):
        row_re = jnp.where(rel_row == tap_index, weight_re[:, tap_index : tap_index + 1], row_re)
        row_im = jnp.where(rel_row == tap_index, weight_im[:, tap_index : tap_index + 1], row_im)
        col_table = jnp.where(rel_col == tap_index, taps_low[tap_index], col_table)
    row_table = jnp.concatenate([row_re, row_im], axis=1)
    return totals + lax.dot_general(
        row_table, col_table, (((0,), (0,)), ((), ())), preferred_element_type=jnp.float32
    )


def local(visibility, target, offset, taps, w_plane):
    tiles = lax.axis_size("tile")
    planes = lax.axis_size("plane")
    devices = tiles * planes
    vis_dev = visibility.shape[1]
    capacity = 2 * vis_dev // devices
    slot_total = devices * capacity
    band = G // tiles
    columns = G // tiles
    kernel_len = taps.shape[0]
    band_rows = band + kernel_len - 1
    destination = target[:, 0]
    onehot = (destination[:, None] == jnp.arange(devices, dtype=jnp.int32)[None, :]).astype(
        jnp.int32
    )
    rank = jnp.sum(jnp.cumsum(onehot, axis=0) * onehot, axis=1) - 1
    slot = destination * capacity + rank
    payload = jnp.stack([visibility[0], visibility[1], offset.astype(jnp.float32) + 1.0])
    outgoing = jnp.zeros((3, slot_total), jnp.float32).at[:, slot].set(payload)
    received = lax.all_to_all(outgoing, ("plane", "tile"), split_axis=1, concat_axis=1, tiled=True)
    block_len = min(512, slot_total)
    empty = jnp.zeros((2 * band_rows, G), jnp.float32)

    def grid_step(index, totals):
        return grid_block(received, taps, index * block_len, block_len, band_rows, totals)

    gridded = lax.fori_loop(0, slot_total // block_len, grid_step, empty)
    gridded = gridded.reshape(2, band_rows, G)
    incoming = shifted(gridded[:, band:], "tile", 1)
    grid_band = gridded[:, :band].at[:, : kernel_len - 1].add(incoming)
    col_re, col_im = transform_last(grid_band[0], grid_band[1])
    stacked = jnp.stack([col_re, col_im]).reshape(2, band, tiles, columns)
    exchanged = lax.all_to_all(stacked, "tile", split_axis=2, concat_axis=1, tiled=True)
    item_count = exchanged.shape[3]
    rows_re, rows_im = transform_first(
        exchanged[0].reshape(G, item_count), exchanged[1].reshape(G, item_count)
    )
    image_parts = jnp.stack([rows_re, rows_im]).reshape(2, G, 1, item_count).reshape(2, G, columns)
    line_pos = jnp.arange(G, dtype=jnp.int32)
    column_pos = lax.axis_index("tile") * columns + jnp.arange(columns, dtype=jnp.int32)
    cos_row = direction(line_pos, G)
    cos_col = direction(column_pos, G)
    n_minus = (
        jnp.sqrt(1.0 - cos_row[:, None] * cos_row[:, None] - cos_col[None, :] * cos_col[None, :])
        - 1.0
    )
    phase = 2.0 * math.pi * w_plane[0] * n_minus
    screened = jnp.cos(phase) * image_parts[0] - jnp.sin(phase) * image_parts[1]
    summed = lax.psum_scatter(screened, "plane", scatter_dimension=0, tiled=True)
    return summed * (1.0 / math.sqrt(vis_dev * devices))


def solution(mesh):
    return jax.shard_map(
        local,
        mesh=mesh,
        in_specs=(
            P(None, ("plane", "tile")),
            P(("plane", "tile"), None),
            P(("plane", "tile")),
            P(),
            P("plane"),
        ),
        out_specs=P("plane", "tile"),
        check_vma=False,
    )
```

profile of v0, /device:TPU:0, one launch (start us, length us, event | category | flops | bytes accessed | tf_op | source)
XLA Modules:
  0.0 1112.9 jit_solution(1792978015275601666)
XLA Ops:
  7.3 9.1 reduce-window.6
  20.4 6.1 scatter_custom_fusion
  27.7 7.3 all-to-all-start
  35.7 6.7 all-to-all-done
  42.5 216.9 %while.18 = (s32[]{:T(128)}, f32[1038,4096]{1,0:T(8,128)}, f32[3,4096]{1,0:T(4,128)S(1)}, f32[8]{0:T(128)}, bf16[8]{0:T(256)(128)(2,1)S(1)}, /*index=5*/s32[]{:T...) while((s32[]{:T(128)}, f32[1038,4096]{1,0:T(8,128)}, f32[3,4096]{1,0:T(4,128)S(1)}, ...), condition=%wide.region_5.6_spmd.clone, body=%wide.region_4.5_spmd.clone.sunk | while | flops 4429704192 | bytes 36240668 | solution.py:135
  46.1 20.6 %select_add_fusion.2 = f32[1038,4096]{1,0:T(8,128)} fusion(f32[1038,4096]{1,0:T(8,128)} %get-tuple-element.356, pred[]{:T(512)S(6)} %compare.38, s32[512]{0:T(512)S(1)} %get-tuple-element.312, bf16[]{:T(256)} %bitcast.127, bf16[]{:T(256)} %bitcast.128, bf16[]{:T(256)} %bitcast.129, bf16[]{:T(256)} %bitcast.130, bf16[]{:T(256)} %bitcast.131, ...), kind=kOutput, calls=%fused_computation.1.clone.1 | convolution fusion | flops 4423036928 | bytes 35078160 | tf_op jit(solution)/shard_map/while/body/eval_jaxpr/dot_general | solution.py:104
  67.7 1.9 fusion.257
  70.2 23.9 %select_add_fusion.2 = f32[1038,4096]{1,0:T(8,128)} fusion(f32[1038,4096]{1,0:T(8,128)} %get-tuple-element.356, pred[]{:T(512)S(6)} %compare.38, s32[512]{0:T(512)S(1)} %get-tuple-element.312, bf16[]{:T(256)} %bitcast.127, bf16[]{:T(256)} %bitcast.128, bf16[]{:T(256)} %bitcast.129, bf16[]{:T(256)} %bitcast.130, bf16[]{:T(256)} %bitcast.131, ...), kind=kOutput, calls=%fused_computation.1.clone.1 | convolution fusion | flops 4423036928 | bytes 35078160 | tf_op jit(solution)/shard_map/while/body/eval_jaxpr/dot_general | solution.py:104
  95.2 1.9 fusion.257
  97.7 23.9 %select_add_fusion.2 = f32[1038,4096]{1,0:T(8,128)} fusion(f32[1038,4096]{1,0:T(8,128)} %get-tuple-element.356, pred[]{:T(512)S(6)} %compare.38, s32[512]{0:T(512)S(1)} %get-tuple-element.312, bf16[]{:T(256)} %bitcast.127, bf16[]{:T(256)} %bitcast.128, bf16[]{:T(256)} %bitcast.129, bf16[]{:T(256)} %bitcast.130, bf16[]{:T(256)} %bitcast.131, ...), kind=kOutput, calls=%fused_computation.1.clone.1 | convolution fusion | flops 4423036928 | bytes 35078160 | tf_op jit(solution)/shard_map/while/body/eval_jaxpr/dot_general | solution.py:104
  125.3 23.9 %select_add_fusion.2 = f32[1038,4096]{1,0:T(8,128)} fusion(f32[1038,4096]{1,0:T(8,128)} %get-tuple-element.356, pred[]{:T(512)S(6)} %compare.38, s32[512]{0:T(512)S(1)} %get-tuple-element.312, bf16[]{:T(256)} %bitcast.127, bf16[]{:T(256)} %bitcast.128, bf16[]{:T(256)} %bitcast.129, bf16[]{:T(256)} %bitcast.130, bf16[]{:T(256)} %bitcast.131, ...), kind=kOutput, calls=%fused_computation.1.clone.1 | convolution fusion | flops 4423036928 | bytes 35078160 | tf_op jit(solution)/shard_map/while/body/eval_jaxpr/dot_general | solution.py:104
  152.8 23.9 %select_add_fusion.2 = f32[1038,4096]{1,0:T(8,128)} fusion(f32[1038,4096]{1,0:T(8,128)} %get-tuple-element.356, pred[]{:T(512)S(6)} %compare.38, s32[512]{0:T(512)S(1)} %get-tuple-element.312, bf16[]{:T(256)} %bitcast.127, bf16[]{:T(256)} %bitcast.128, bf16[]{:T(256)} %bitcast.129, bf16[]{:T(256)} %bitcast.130, bf16[]{:T(256)} %bitcast.131, ...), kind=kOutput, calls=%fused_computation.1.clone.1 | convolution fusion | flops 4423036928 | bytes 35078160 | tf_op jit(solution)/shard_map/while/body/eval_jaxpr/dot_general | solution.py:104
  180.4 23.9 %select_add_fusion.2 = f32[1038,4096]{1,0:T(8,128)} fusion(f32[1038,4096]{1,0:T(8,128)} %get-tuple-element.356, pred[]{:T(512)S(6)} %compare.38, s32[512]{0:T(512)S(1)} %get-tuple-element.312, bf16[]{:T(256)} %bitcast.127, bf16[]{:T(256)} %bitcast.128, bf16[]{:T(256)} %bitcast.129, bf16[]{:T(256)} %bitcast.130, bf16[]{:T(256)} %bitcast.131, ...), kind=kOutput, calls=%fused_computation.1.clone.1 | convolution fusion | flops 4423036928 | bytes 35078160 | tf_op jit(solution)/shard_map/while/body/eval_jaxpr/dot_general | solution.py:104
  207.9 23.9 %select_add_fusion.2 = f32[1038,4096]{1,0:T(8,128)} fusion(f32[1038,4096]{1,0:T(8,128)} %get-tuple-element.356, pred[]{:T(512)S(6)} %compare.38, s32[512]{0:T(512)S(1)} %get-tuple-element.312, bf16[]{:T(256)} %bitcast.127, bf16[]{:T(256)} %bitcast.128, bf16[]{:T(256)} %bitcast.129, bf16[]{:T(256)} %bitcast.130, bf16[]{:T(256)} %bitcast.131, ...), kind=kOutput, calls=%fused_computation.1.clone.1 | convolution fusion | flops 4423036928 | bytes 35078160 | tf_op jit(solution)/shard_map/while/body/eval_jaxpr/dot_general | solution.py:104
  235.4 23.9 %select_add_fusion.2 = f32[1038,4096]{1,0:T(8,128)} fusion(f32[1038,4096]{1,0:T(8,128)} %get-tuple-element.356, pred[]{:T(512)S(6)} %compare.38, s32[512]{0:T(512)S(1)} %get-tuple-element.312, bf16[]{:T(256)} %bitcast.127, bf16[]{:T(256)} %bitcast.128, bf16[]{:T(256)} %bitcast.129, bf16[]{:T(256)} %bitcast.130, bf16[]{:T(256)} %bitcast.131, ...), kind=kOutput, calls=%fused_computation.1.clone.1 | convolution fusion | flops 4423036928 | bytes 35078160 | tf_op jit(solution)/shard_map/while/body/eval_jaxpr/dot_general | solution.py:104
  259.4 13.3 %reshape.237 = f32[2,519,4096]{2,1,0:T(8,128)} reshape(f32[1038,4096]{1,0:T(8,128)} %get-tuple-element.158) | data formatting | bytes 34013184 | tf_op jit(solution)/shard_map/reshape | solution.py:136
  274.1 11.5 %slice.405 = f32[2,512,4096]{2,1,0:T(8,128)} slice(f32[2,519,4096]{2,1,0:T(8,128)} %reshape.237), slice={[0:2], [0:512], [0:4096]} | slice | bytes 33554432 | tf_op jit(solution)/shard_map/slice | solution.py:138
  288.4 10.1 slice_bitcast_fusion
  298.5 5.2 copy.69
  303.7 9.5 fusion.145
  313.2 9.7 fusion.149
  324.8 9.5 fusion.143
  334.3 19.1 %subtract_bitcast_fusion.1 = (f32[512,32,128]{2,1,0:T(8,128)}, f32[512,32,128]{2,1,0:T(8,128)}) fusion(f32[32,128]{1,0:T(8,128)S(1)} %get-tuple-element.239, f32[32,128]{1,0:T(8,128)S(1)} %get-tuple-element.240, f32[32,512,128]{2,0,1:T(8,128)} %fusion.143, f32[32,512,128]{2,0,1:T(8,128)} %fusion.149, f32[32,512,128]{2,0,1:T(8,128)} %fusion.145, ...), kind=kOutput, calls=%fused_computation.116 | convolution fusion | flops 822097920 | bytes 50364416 | tf_op jit(solution)/shard_map/rab,ak->rkb/dot_general | solution.py:41
  353.4 21.6 %fusion.84 = f32[128,512,32]{1,0,2:T(8,128)} fusion(f32[512,32,128]{2,1,0:T(8,128)} %get-tuple-element.234), kind=kOutput, calls=%fused_computation.135 | convolution fusion | flops 3221454848 | bytes 16777216 | tf_op jit(solution)/shard_map/rkb,bq->rqk/dot_general | solution.py:51
  375.0 16.1 %fusion.82 = f32[128,512,32]{1,0,2:T(8,128)S(1)} fusion(f32[512,32,128]{2,1,0:T(8,128)S(1)} %copy-done.2), kind=kOutput, calls=%fused_computation.133 | convolution fusion | flops 3221454848 | bytes 16777216 | tf_op jit(solution)/shard_map/rkb,bq->rqk/dot_general | solution.py:54
  391.1 15.9 %subtract_bitcast_fusion = f32[512,128,32]{0,1,2:T(8,128)} fusion(f32[128,512,32]{1,0,2:T(8,128)} %fusion.84, f32[512,32,128]{2,1,0:T(8,128)S(1)} %bitcast.140), kind=kOutput, calls=%fused_computation.114 | convolution fusion | flops 3223552000 | bytes 25165824 | tf_op jit(solution)/shard_map/rkb,bq->rqk/dot_general | solution.py:51
  407.0 11.5 %copy.48 = f32[512,128,32]{0,2,1:T(8,128)} copy(f32[512,128,32]{0,1,2:T(8,128)} %subtract_bitcast_fusion) | data formatting | bytes 16777216 | tf_op jit(solution)/shard_map/sub | solution.py:51
  418.5 13.7 %add_bitcast_fusion = f32[512,128,32]{0,1,2:T(8,128)} fusion(f32[128,512,32]{1,0,2:T(8,128)S(1)} %fusion.82, f32[512,32,128]{2,1,0:T(8,128)S(1)} %bitcast.140), kind=kOutput, calls=%fused_computation.113 | convolution fusion | flops 3223552000 | bytes 25165824 | tf_op jit(solution)/shard_map/rkb,bq->rqk/dot_general | solution.py:54
  432.2 8.4 copy.51
  440.6 1.9 pad_maximum_fusion
  442.6 6.2 copy.52
  448.7 5.8 all-to-all-start.1
  455.4 362.7 %all-to-all-done.1 = f32[2,512,8,512]{1,3,0,2:T(8,128)} async-done(((f32[2,512,8,512]{1,3,0,2:T(8,128)}), f32[2,512,8,512]{1,3,0,2:T(8,128)}, u32[]{:S(2)}, u32[]{:S(2)}) %all-to-all-start.1) | async-done | bytes 16777248 | tf_op jit(solution)/shard_map/all_to_all | solution.py:141
  818.1 17.6 %copy.53 = f32[2,512,8,512]{3,1,2,0:T(8,128)} copy(f32[2,512,8,512]{1,3,0,2:T(8,128)} %all-to-all-done.1) | data formatting | bytes 33554432 | tf_op jit(solution)/shard_map/all_to_all | solution.py:141
  835.7 6.9 fusion.245
  842.6 13.2 %fusion.74 = f32[32,128,512]{2,0,1:T(8,128)} fusion(f32[32,128,512]{2,1,0:T(8,128)S(1)} %bitcast.145), kind=kOutput, calls=%fused_computation.125 | convolution fusion | flops 805320704 | bytes 16777216 | tf_op jit(solution)/shard_map/abc,ak->kbc/dot_general | solution.py:69
  855.8 13.4 %fusion.76 = f32[32,128,512]{2,0,1:T(8,128)} fusion(f32[32,128,512]{2,1,0:T(8,128)S(1)} %bitcast.146), kind=kOutput, calls=%fused_computation.127 | convolution fusion | flops 805320704 | bytes 16777216 | tf_op jit(solution)/shard_map/abc,ak->kbc/dot_general | solution.py:66
  869.3 13.2 %fusion.80 = f32[32,128,512]{2,0,1:T(8,128)} fusion(f32[32,128,512]{2,1,0:T(8,128)S(1)} %bitcast.147), kind=kOutput, calls=%fused_computation.131 | convolution fusion | flops 805320704 | bytes 16777216 | tf_op jit(solution)/shard_map/abc,ak->kbc/dot_general | solution.py:66
  882.4 24.2 %multiply_subtract_fusion = (f32[32,128,512]{2,0,1:T(8,128)}, f32[32,128,512]{2,0,1:T(8,128)}) fusion(f32[32,128]{0,1:T(8,128)S(1)} %copy.59, f32[32,128]{0,1:T(8,128)S(1)} %copy.56, f32[32,128,512]{2,0,1:T(8,128)} %fusion.74, f32[32,128,512]{2,0,1:T(8,128)} %fusion.80, f32[32,128,512]{2,0,1:T(8,128)} %fusion.76, f32[32,128,512]{2,1,0:T(8,128)} %bitcast.148), kind=kOutput, calls=%fused_computation.112 | convolution fusion | flops 822097920 | bytes 50364416 | tf_op jit(solution)/shard_map/abc,ak->kbc/dot_general | solution.py:69
  906.7 17.0 %fusion.68 = f32[128,32,512]{2,0,1:T(8,128)S(1)} fusion(f32[32,128,512]{2,0,1:T(8,128)} %get-tuple-element.232), kind=kOutput, calls=%fused_computation.119 | convolution fusion | flops 3221454848 | bytes 16777216 | tf_op jit(solution)/shard_map/kbc,bq->qkc/dot_general | solution.py:76
  923.7 13.6 %fusion.66 = f32[128,32,512]{2,0,1:T(8,128)} fusion(f32[32,128,512]{2,0,1:T(8,128)S(1)} %copy-done), kind=kOutput, calls=%fused_computation.117 | convolution fusion | flops 3221454848 | bytes 16777216 | tf_op jit(solution)/shard_map/kbc,bq->qkc/dot_general | solution.py:79
  937.3 13.6 %fusion.94 = f32[128,32,512]{2,0,1:T(8,128)} fusion(f32[128,32,512]{2,0,1:T(8,128)S(1)} %fusion.68, f32[32,128,512]{2,0,1:T(8,128)S(1)} %bitcast.138), kind=kOutput, calls=%fused_computation.141 | convolution fusion | flops 3223552000 | bytes 25165824 | tf_op jit(solution)/shard_map/kbc,bq->qkc/dot_general | solution.py:76
  950.9 8.2 copy.62
  959.1 15.6 %fusion.97 = f32[128,32,512]{2,0,1:T(8,128)} fusion(f32[128,32,512]{2,0,1:T(8,128)} %fusion.66, f32[32,128,512]{2,0,1:T(8,128)S(1)} %bitcast.138), kind=kOutput, calls=%fused_computation.142 | convolution fusion | flops 3223552000 | bytes 25165824 | tf_op jit(solution)/shard_map/kbc,bq->qkc/dot_general | solution.py:79
  974.8 8.2 copy.65
  983.0 36.1 %fusion.65 = f32[4096,512]{1,0:T(8,128)} fusion(f32[128,32,512]{2,1,0:T(8,128)S(1)} %copy.65, f32[128,32,512]{2,1,0:T(8,128)S(1)} %copy.62, f32[512]{0:T(512)S(1)} %fusion.178, f32[4096]{0:T(1024)S(1)} %fusion.134, f32[]{:T(128)} %bitcast), kind=kLoop, calls=%fused_computation.109 | loop fusion | flops 12582912 | bytes 25184260 | tf_op jit(solution)/shard_map/sub | solution.py:156
  1019.1 83.6 %reduce-scatter.2.cloned.1.call-done = f32[1024,512]{1,0:T(8,128)} async-done(((f32[4096,512]{1,0:T(8,128)}), f32[1024,512]{1,0:T(8,128)}) %reduce-scatter.2.cloned.1.call-update) | async-done | bytes 2097168 | tf_op jit(solution)/shard_map/reduce_scatter | solution.py:157
  1102.7 3.1 broadcast_multiply_fusion
  (109 shorter events, 37.8 us)
Async XLA Ops:
  27.7 14.7 %all-to-all-start = ((f32[3,32,128]{2,0,1:T(4,128)}), f32[3,32,128]{2,0,1:T(4,128)S(1)}, u32[]{:S(2)}, u32[]{:S(2)}) async-start(f32[3,32,128]{2,0,1:T(4,128)} %copy.45), calls=%async_computation | async-start | bytes 131072 | tf_op jit(solution)/shard_map/all_to_all | solution.py:128
  273.6 12.0 %collective-permute-start = (f32[2,7,4096]{2,1,0:T(8,128)S(1)}, f32[2,7,4096]{2,1,0:T(8,128)S(1)}, u32[]{:S(2)}, u32[]{:S(2)}) collective-permute-start(f32[2,7,4096]{2,1,0:T(8,128)S(1)} %slice.407), channel_id=1, source_target_pairs={{0,1},{1,2},{2,3},{3,4},{4,5},{5,6},{6,7},{7,0},{8,9},{9,10},{10,1... | collective-permute-start | bytes 688136 | tf_op jit(solution)/shard_map/ppermute | solution.py:13
  324.8 9.5 copy-start.1
  353.4 21.6 %copy-start.2 = (f32[512,32,128]{2,1,0:T(8,128)S(1)}, f32[512,32,128]{2,1,0:T(8,128)}, u32[]{:S(2)}) copy-start(f32[512,32,128]{2,1,0:T(8,128)} %get-tuple-element.234) | copy-start | bytes 25165828
  353.4 37.7 %slice-start.2 = ((s8[8388608]{0:T(1024)(128)(4,1)}), s8[4194304]{0:T(1024)(128)(4,1)S(1)}, s32[]{:S(2)}) async-start(s8[8388608]{0:T(1024)(128)(4,1)} %bitcast.139), calls=%async_computation.6 | async-start | bytes 8388608
  375.0 16.1 %slice-start.3 = ((s8[8388608]{0:T(1024)(128)(4,1)}), s8[4194304]{0:T(1024)(128)(4,1)S(1)}, s32[]{:S(2)}) async-start(s8[8388608]{0:T(1024)(128)(4,1)} %bitcast.139), calls=%async_computation.7 | async-start | bytes 8388608
  432.2 8.4 copy-start.4
  448.7 369.4 %all-to-all-start.1 = ((f32[2,512,8,512]{1,3,0,2:T(8,128)}), f32[2,512,8,512]{1,3,0,2:T(8,128)}, u32[]{:S(2)}, u32[]{:S(2)}) async-start(f32[2,512,8,512]{1,3,0,2:T(8,128)} %copy.52), calls=%async_computation.1 | async-start | bytes 33554432 | tf_op jit(solution)/shard_map/all_to_all | solution.py:141
  454.5 648.2 %reduce-scatter.2.cloned.1.call-start = ((), (), s32[]{:S(2)}) async-start(), calls=%async_computation.3 | async-start | bytes 10485760 | tf_op jit(solution)/shard_map/reduce_scatter | solution.py:157
  842.6 26.7 %copy-start.3 = (f32[1,8,512,1,512]{4,2,1,3,0:T(8,128)}, f32[1,8,512,1,512]{4,2,1,3,0:T(8,128)S(1)}, u32[]{:S(2)}) copy-start(f32[1,8,512,1,512]{4,2,1,3,0:T(8,128)S(1)} %get-tuple-element.236) | copy-start | bytes 25165828
  906.7 17.0 %copy-start = (f32[32,128,512]{2,0,1:T(8,128)S(1)}, f32[32,128,512]{2,0,1:T(8,128)}, u32[]{:S(2)}) copy-start(f32[32,128,512]{2,0,1:T(8,128)} %get-tuple-element.232) | copy-start | bytes 25165828
  906.7 30.6 %slice-start = ((s8[8388608]{0:T(1024)(128)(4,1)}), s8[4194304]{0:T(1024)(128)(4,1)S(1)}, s32[]{:S(2)}) async-start(s8[8388608]{0:T(1024)(128)(4,1)} %bitcast.137), calls=%async_computation.4 | async-start | bytes 8388608
  923.7 13.6 %slice-start.1 = ((s8[8388608]{0:T(1024)(128)(4,1)}), s8[4194304]{0:T(1024)(128)(4,1)S(1)}, s32[]{:S(2)}) async-start(s8[8388608]{0:T(1024)(128)(4,1)} %bitcast.137), calls=%async_computation.5 | async-start | bytes 8388608
Sparse Core Ops, SparseCore 0:
  1019.2 83.4 reduce-scatter.1
where the time goes:
time: 1120 us; the launch traced here: 1110 us
  waiting for transfers between devices  453 us (40%)
  matrix products  427 us (38%)
  local copies, waits for them, and re-layouts  127 us (11%)
  other arithmetic  77.7 us (7%)
  between operations  14.6 us (1%)
  starting transfers between devices  13.5 us (1%)
    all_to_all x1, waiting for transfers between devices, local(): lax.all_to_all(stacked, 'tile', split_axis=2, concat_axis=1, tiled=True)  363 us
    dot_general x8, matrix products, grid_block(): lax.dot_general(row_table, col_table, (((0,), (0,)), ((), ())), preferred...  188 us
    reduce_scatter x1, waiting for transfers between devices, local(): lax.psum_scatter(screened, 'plane', scatter_dimension=0, tiled=True)  83.6 us
    sub x1, other arithmetic, local(): screened = jnp.cos(phase) * image_parts[0] - jnp.sin(phase) * image_parts[1]  36.1 us
    dot_general x1, matrix products, transform_first(): jnp.einsum('abc,ak->kbc', real_grid, sin_one, precision=HIGHEST)  24.2 us
  transfers between devices with their start and end apart: 4, of which 3 were waited for; matrix products, arithmetic and copies ran while one was open for 1% of the time, Pallas kernels for 0%

commit v1 on v0

--- a/solution.py
+++ b/solution.py
@@ -6,6 +6,18 @@
 
 G = 4096
 HIGHEST = lax.Precision.HIGHEST
+
+
+def split_up(value, dim, size):
+    shape = value.shape
+    blocks = value.reshape(*shape[:dim], size, shape[dim] // size, *shape[dim + 1 :])
+    return jnp.moveaxis(blocks, dim, 0)
+
+
+def in_order(blocks, dim):
+    lengths = list(blocks.shape[1:])
+    lengths[dim] *= blocks.shape[0]
+    return jnp.moveaxis(blocks, 0, dim).reshape(lengths)
 
 
 def shifted(x, axis, by):
@@ -138,7 +150,14 @@
     grid_band = gridded[:, :band].at[:, : kernel_len - 1].add(incoming)
     col_re, col_im = transform_last(grid_band[0], grid_band[1])
     stacked = jnp.stack([col_re, col_im]).reshape(2, band, tiles, columns)
-    exchanged = lax.all_to_all(stacked, "tile", split_axis=2, concat_axis=1, tiled=True)
+    size, index_2 = (lax.axis_size("tile"), lax.axis_index("tile"))
+    tiles_2 = split_up(stacked, 2, size)
+    done = [tiles_2[index_2]]
+    for hop in range(1, size):
+        sent = tiles_2[index_2 ^ hop]
+        done.append(lax.ppermute(sent, "tile", [(i_2, i_2 ^ hop) for i_2 in range(size)]))
+    tiles_2 = jnp.stack(done)[index_2 ^ jnp.arange(size)]
+    exchanged = in_order(tiles_2, 1)
     item_count = exchanged.shape[3]
     rows_re, rows_im = transform_first(
         exchanged[0].reshape(G, item_count), exchanged[1].reshape(G, item_count)

time: 1120 us -> 1120 us (level)
  waiting for transfers between devices: 453 us -> 411 us
  local copies, waits for them, and re-layouts: 127 us -> 160 us
    all_to_all x1 -> x0, waiting for transfers between devices: 363 us -> none  [local(): lax.all_to_all(stacked, 'tile', split_axis=2, concat_axis=1, tiled=True)]
    ppermute x0 -> x7, waiting for transfers between devices: none -> 236 us  [local(): lax.ppermute(sent, 'tile', [(i_2, i_2 ^ hop) for i_2 in range(size)])]
    reduce_scatter x1, waiting for transfers between devices: 83.6 us -> 169 us  [local(): lax.psum_scatter(screened, 'plane', scatter_dimension=0, tiled=True)]
    unnamed x21 -> x30, local copies, waits for them, and re-layouts: 17.1 us -> 40.1 us
    all_to_all x1 -> x0, local copies, waits for them, and re-layouts: 17.6 us -> none  [local(): lax.all_to_all(stacked, 'tile', split_axis=2, concat_axis=1, tiled=True)]
    another operation x3 -> x11, local copies, waits for them, and re-layouts: 6.54 us -> 24.1 us  [the longest x1 6.18 us: local(): stacked = jnp.stack([col_re, col_im]).reshape(2, band, tiles, columns)]
    gather x0 -> x1, local copies, waits for them, and re-layouts: none -> 13.9 us  [local(): tiles_2 = jnp.stack(done)[index_2 ^ jnp.arange(size)]]
  transfers between devices with their start and end apart: 4 -> 10, of which waited for: 3 -> 5; matrix products, arithmetic and copies ran while one was open for 1% -> 5% of each run, Pallas kernels for 0% -> 0%
where the time goes in v1:
time: 1120 us; the launch traced here: 1110 us
  matrix products  424 us (38%)
  waiting for transfers between devices  411 us (37%)
  local copies, waits for them, and re-layouts  160 us (14%)
  other arithmetic  85.5 us (8%)
  starting transfers between devices  15.9 us (1%)
  between operations  14.8 us (1%)
    ppermute x7, waiting for transfers between devices, local(): lax.ppermute(sent, 'tile', [(i_2, i_2 ^ hop) for i_2 in range(size)])  236 us
    dot_general x8, matrix products, grid_block(): lax.dot_general(row_table, col_table, (((0,), (0,)), ((), ())), preferred...  188 us
    reduce_scatter x1, waiting for transfers between devices, local(): lax.psum_scatter(screened, 'plane', scatter_dimension=0, tiled=True)  169 us
    unnamed x30, local copies, waits for them, and re-layouts  40.1 us
    sub x1, other arithmetic, local(): screened = jnp.cos(phase) * image_parts[0] - jnp.sin(phase) * image_parts[1]  36.1 us
    dot_general x1, matrix products, transform_first(): jnp.einsum('abc,ak->kbc', real_grid, sin_one, precision=HIGHEST)  24.5 us
    another operation x10, local copies, waits for them, and re-layouts  22.6 us
  transfers between devices with their start and end apart: 10, of which 5 were waited for; matrix products, arithmetic and copies ran while one was open for 5% of the time, Pallas kernels for 0%

profile of v1, /device:TPU:0, one launch (start us, length us, event | category | flops | bytes accessed | tf_op | source)
XLA Modules:
  0.0 1112.5 jit_solution(12979587282691348988)
XLA Ops:
  7.3 9.1 reduce-window.6
  20.4 6.1 scatter_custom_fusion
  27.7 7.3 all-to-all-start
  35.8 6.7 all-to-all-done
  42.5 216.9 %while.18 = (s32[]{:T(128)}, f32[1038,4096]{1,0:T(8,128)}, f32[3,4096]{1,0:T(4,128)S(1)}, f32[8]{0:T(128)}, bf16[8]{0:T(256)(128)(2,1)S(1)}, /*index=5*/s32[]{:T...) while((s32[]{:T(128)}, f32[1038,4096]{1,0:T(8,128)}, f32[3,4096]{1,0:T(4,128)S(1)}, ...), condition=%wide.region_5.6_spmd.clone, body=%wide.region_4.5_spmd.clone.sunk | while | flops 4429704192 | bytes 36240668 | solution.py:147
  46.1 20.6 %select_add_fusion.2 = f32[1038,4096]{1,0:T(8,128)} fusion(f32[1038,4096]{1,0:T(8,128)} %get-tuple-element.364, pred[]{:T(512)S(6)} %compare.38, s32[512]{0:T(512)S(1)} %get-tuple-element.320, bf16[]{:T(256)} %bitcast.153, bf16[]{:T(256)} %bitcast.154, bf16[]{:T(256)} %bitcast.155, bf16[]{:T(256)} %bitcast.156, bf16[]{:T(256)} %bitcast.157, ...), kind=kOutput, calls=%fused_computation.2.clone.1 | convolution fusion | flops 4423036928 | bytes 35078160 | tf_op jit(solution)/shard_map/while/body/eval_jaxpr/dot_general | solution.py:116
  70.2 23.9 %select_add_fusion.2 = f32[1038,4096]{1,0:T(8,128)} fusion(f32[1038,4096]{1,0:T(8,128)} %get-tuple-element.364, pred[]{:T(512)S(6)} %compare.38, s32[512]{0:T(512)S(1)} %get-tuple-element.320, bf16[]{:T(256)} %bitcast.153, bf16[]{:T(256)} %bitcast.154, bf16[]{:T(256)} %bitcast.155, bf16[]{:T(256)} %bitcast.156, bf16[]{:T(256)} %bitcast.157, ...), kind=kOutput, calls=%fused_computation.2.clone.1 | convolution fusion | flops 4423036928 | bytes 35078160 | tf_op jit(solution)/shard_map/while/body/eval_jaxpr/dot_general | solution.py:116
  97.7 23.9 %select_add_fusion.2 = f32[1038,4096]{1,0:T(8,128)} fusion(f32[1038,4096]{1,0:T(8,128)} %get-tuple-element.364, pred[]{:T(512)S(6)} %compare.38, s32[512]{0:T(512)S(1)} %get-tuple-element.320, bf16[]{:T(256)} %bitcast.153, bf16[]{:T(256)} %bitcast.154, bf16[]{:T(256)} %bitcast.155, bf16[]{:T(256)} %bitcast.156, bf16[]{:T(256)} %bitcast.157, ...), kind=kOutput, calls=%fused_computation.2.clone.1 | convolution fusion | flops 4423036928 | bytes 35078160 | tf_op jit(solution)/shard_map/while/body/eval_jaxpr/dot_general | solution.py:116
  125.3 23.9 %select_add_fusion.2 = f32[1038,4096]{1,0:T(8,128)} fusion(f32[1038,4096]{1,0:T(8,128)} %get-tuple-element.364, pred[]{:T(512)S(6)} %compare.38, s32[512]{0:T(512)S(1)} %get-tuple-element.320, bf16[]{:T(256)} %bitcast.153, bf16[]{:T(256)} %bitcast.154, bf16[]{:T(256)} %bitcast.155, bf16[]{:T(256)} %bitcast.156, bf16[]{:T(256)} %bitcast.157, ...), kind=kOutput, calls=%fused_computation.2.clone.1 | convolution fusion | flops 4423036928 | bytes 35078160 | tf_op jit(solution)/shard_map/while/body/eval_jaxpr/dot_general | solution.py:116
  152.8 23.9 %select_add_fusion.2 = f32[1038,4096]{1,0:T(8,128)} fusion(f32[1038,4096]{1,0:T(8,128)} %get-tuple-element.364, pred[]{:T(512)S(6)} %compare.38, s32[512]{0:T(512)S(1)} %get-tuple-element.320, bf16[]{:T(256)} %bitcast.153, bf16[]{:T(256)} %bitcast.154, bf16[]{:T(256)} %bitcast.155, bf16[]{:T(256)} %bitcast.156, bf16[]{:T(256)} %bitcast.157, ...), kind=kOutput, calls=%fused_computation.2.clone.1 | convolution fusion | flops 4423036928 | bytes 35078160 | tf_op jit(solution)/shard_map/while/body/eval_jaxpr/dot_general | solution.py:116
  180.4 23.9 %select_add_fusion.2 = f32[1038,4096]{1,0:T(8,128)} fusion(f32[1038,4096]{1,0:T(8,128)} %get-tuple-element.364, pred[]{:T(512)S(6)} %compare.38, s32[512]{0:T(512)S(1)} %get-tuple-element.320, bf16[]{:T(256)} %bitcast.153, bf16[]{:T(256)} %bitcast.154, bf16[]{:T(256)} %bitcast.155, bf16[]{:T(256)} %bitcast.156, bf16[]{:T(256)} %bitcast.157, ...), kind=kOutput, calls=%fused_computation.2.clone.1 | convolution fusion | flops 4423036928 | bytes 35078160 | tf_op jit(solution)/shard_map/while/body/eval_jaxpr/dot_general | solution.py:116
  207.9 23.9 %select_add_fusion.2 = f32[1038,4096]{1,0:T(8,128)} fusion(f32[1038,4096]{1,0:T(8,128)} %get-tuple-element.364, pred[]{:T(512)S(6)} %compare.38, s32[512]{0:T(512)S(1)} %get-tuple-element.320, bf16[]{:T(256)} %bitcast.153, bf16[]{:T(256)} %bitcast.154, bf16[]{:T(256)} %bitcast.155, bf16[]{:T(256)} %bitcast.156, bf16[]{:T(256)} %bitcast.157, ...), kind=kOutput, calls=%fused_computation.2.clone.1 | convolution fusion | flops 4423036928 | bytes 35078160 | tf_op jit(solution)/shard_map/while/body/eval_jaxpr/dot_general | solution.py:116
  235.4 23.9 %select_add_fusion.2 = f32[1038,4096]{1,0:T(8,128)} fusion(f32[1038,4096]{1,0:T(8,128)} %get-tuple-element.364, pred[]{:T(512)S(6)} %compare.38, s32[512]{0:T(512)S(1)} %get-tuple-element.320, bf16[]{:T(256)} %bitcast.153, bf16[]{:T(256)} %bitcast.154, bf16[]{:T(256)} %bitcast.155, bf16[]{:T(256)} %bitcast.156, bf16[]{:T(256)} %bitcast.157, ...), kind=kOutput, calls=%fused_computation.2.clone.1 | convolution fusion | flops 4423036928 | bytes 35078160 | tf_op jit(solution)/shard_map/while/body/eval_jaxpr/dot_general | solution.py:116
  259.4 13.3 %reshape.268 = f32[2,519,4096]{2,1,0:T(8,128)} reshape(f32[1038,4096]{1,0:T(8,128)} %get-tuple-element.158) | data formatting | bytes 34013184 | tf_op jit(solution)/shard_map/reshape | solution.py:148
  274.1 11.5 %slice.407 = f32[2,512,4096]{2,1,0:T(8,128)} slice(f32[2,519,4096]{2,1,0:T(8,128)} %reshape.268), slice={[0:2], [0:512], [0:4096]} | slice | bytes 33554432 | tf_op jit(solution)/shard_map/slice | solution.py:150
  288.4 10.1 slice_bitcast_fusion
  298.5 5.2 copy.103
  303.7 9.5 fusion.153
  313.2 9.7 fusion.157
  324.8 9.5 fusion.151
  334.3 18.7 %subtract_bitcast_fusion.1 = (f32[512,32,128]{2,1,0:T(8,128)}, f32[512,32,128]{2,1,0:T(8,128)}) fusion(f32[32,128]{1,0:T(8,128)S(1)} %get-tuple-element.247, f32[32,128]{1,0:T(8,128)S(1)} %get-tuple-element.248, f32[32,512,128]{2,0,1:T(8,128)} %fusion.151, f32[32,512,128]{2,0,1:T(8,128)} %fusion.157, f32[32,512,128]{2,0,1:T(8,128)} %fusion.153, ...), kind=kOutput, calls=%fused_computation.132 | convolution fusion | flops 822097920 | bytes 50364416 | tf_op jit(solution)/shard_map/rab,ak->rkb/dot_general | solution.py:53
  353.0 18.7 %fusion.82 = f32[128,512,32]{1,0,2:T(8,128)S(1)} fusion(f32[512,32,128]{2,1,0:T(8,128)} %get-tuple-element.234), kind=kOutput, calls=%fused_computation.149 | convolution fusion | flops 3221454848 | bytes 16777216 | tf_op jit(solution)/shard_map/rkb,bq->rqk/dot_general | solution.py:66
  371.8 13.6 %fusion.84 = f32[128,512,32]{1,0,2:T(8,128)} fusion(f32[512,32,128]{2,1,0:T(8,128)S(1)} %copy-done.4), kind=kOutput, calls=%fused_computation.151 | convolution fusion | flops 3221454848 | bytes 16777216 | tf_op jit(solution)/shard_map/rkb,bq->rqk/dot_general | solution.py:63
  385.4 13.9 %add_bitcast_fusion = f32[512,128,32]{0,1,2:T(8,128)} fusion(f32[128,512,32]{1,0,2:T(8,128)S(1)} %fusion.82, f32[512,32,128]{2,1,0:T(8,128)S(1)} %bitcast.170), kind=kOutput, calls=%fused_computation.129 | convolution fusion | flops 3223552000 | bytes 25165824 | tf_op jit(solution)/shard_map/rkb,bq->rqk/dot_general | solution.py:66
  399.2 8.2 copy.79
  407.5 18.9 %subtract_bitcast_fusion = f32[512,128,32]{0,1,2:T(8,128)} fusion(f32[128,512,32]{1,0,2:T(8,128)} %fusion.84, f32[512,32,128]{2,1,0:T(8,128)S(1)} %bitcast.170), kind=kOutput, calls=%fused_computation.130 | convolution fusion | flops 3223552000 | bytes 25165824 | tf_op jit(solution)/shard_map/rkb,bq->rqk/dot_general | solution.py:63
  426.4 8.2 copy.76
  434.7 5.1 fusion.100
  457.1 4.7 fusion.107
  468.1 3.4 collective-permute-start.6
  477.0 101.7 %collective-permute-done.2 = f32[2,512,1,512]{3,1,0,2:T(8,128)} collective-permute-done((f32[2,512,1,512]{3,1,0,2:T(8,128)}, f32[2,512,1,512]{3,1,0,2:T(8,128)}, u32[]{:S(2)}, u32[]{:S(2)}) %collective-permute-start.2) | collective-permute-done | bytes 2097184 | tf_op jit(solution)/shard_map/ppermute | solution.py:158
  588.0 33.8 %collective-permute-done.3 = f32[2,512,1,512]{3,1,0,2:T(8,128)} collective-permute-done((f32[2,512,1,512]{3,1,0,2:T(8,128)}, f32[2,512,1,512]{3,1,0,2:T(8,128)}, u32[]{:S(2)}, u32[]{:S(2)}) %collective-permute-start.3) | collective-permute-done | bytes 2097184 | tf_op jit(solution)/shard_map/ppermute | solution.py:158
  625.0 3.2 bitcast_dynamic-update-slice_fusion.3
  628.1 100.4 %collective-permute-done.5 = f32[2,512,1,512]{3,1,0,2:T(8,128)} collective-permute-done((f32[2,512,1,512]{3,1,0,2:T(8,128)}, f32[2,512,1,512]{3,1,0,2:T(8,128)}, u32[]{:S(2)}, u32[]{:S(2)}) %collective-permute-start.5) | collective-permute-done | bytes 2097184 | tf_op jit(solution)/shard_map/ppermute | solution.py:158
  736.3 13.9 %gather_fusion = f32[8,2,512,512]{3,2,1,0:T(8,128)} fusion(f32[8,2,512,512]{3,2,1,0:T(8,128)} %bitcast.37, s32[1024]{0:T(1024)S(1)} %pad_clamp_fusion), kind=kCustom, calls=%fused_computation | custom fusion | bytes 33554464 | tf_op jit(solution)/shard_map/gather | solution.py:159
  750.2 6.9 fusion.254
  757.1 13.2 %fusion.74 = f32[32,128,512]{2,0,1:T(8,128)} fusion(f32[32,128,512]{2,1,0:T(8,128)S(1)} %bitcast.175), kind=kOutput, calls=%fused_computation.141 | convolution fusion | flops 805320704 | bytes 16777216 | tf_op jit(solution)/shard_map/abc,ak->kbc/dot_general | solution.py:81
  770.3 13.2 %fusion.76 = f32[32,128,512]{2,0,1:T(8,128)} fusion(f32[32,128,512]{2,1,0:T(8,128)S(1)} %bitcast.176), kind=kOutput, calls=%fused_computation.143 | convolution fusion | flops 805320704 | bytes 16777216 | tf_op jit(solution)/shard_map/abc,ak->kbc/dot_general | solution.py:78
  783.6 13.2 %fusion.80 = f32[32,128,512]{2,0,1:T(8,128)} fusion(f32[32,128,512]{2,1,0:T(8,128)S(1)} %bitcast.177), kind=kOutput, calls=%fused_computation.147 | convolution fusion | flops 805320704 | bytes 16777216 | tf_op jit(solution)/shard_map/abc,ak->kbc/dot_general | solution.py:78
  796.7 24.5 %multiply_subtract_fusion = (f32[32,128,512]{2,0,1:T(8,128)}, f32[32,128,512]{2,0,1:T(8,128)}) fusion(f32[32,128]{0,1:T(8,128)S(1)} %copy.93, f32[32,128]{0,1:T(8,128)S(1)} %copy.90, f32[32,128,512]{2,0,1:T(8,128)} %fusion.74, f32[32,128,512]{2,0,1:T(8,128)} %fusion.80, f32[32,128,512]{2,0,1:T(8,128)} %fusion.76, f32[32,128,512]{2,1,0:T(8,128)} %bitcast.178), kind=kOutput, calls=%fused_computation.128 | convolution fusion | flops 822097920 | bytes 50364416 | tf_op jit(solution)/shard_map/abc,ak->kbc/dot_general | solution.py:81
  821.2 17.0 %fusion.68 = f32[128,32,512]{2,0,1:T(8,128)S(1)} fusion(f32[32,128,512]{2,0,1:T(8,128)} %get-tuple-element.232), kind=kOutput, calls=%fused_computation.135 | convolution fusion | flops 3221454848 | bytes 16777216 | tf_op jit(solution)/shard_map/kbc,bq->qkc/dot_general | solution.py:88
  838.3 13.4 %fusion.66 = f32[128,32,512]{2,0,1:T(8,128)} fusion(f32[32,128,512]{2,0,1:T(8,128)S(1)} %copy-done.2), kind=kOutput, calls=%fused_computation.133 | convolution fusion | flops 3221454848 | bytes 16777216 | tf_op jit(solution)/shard_map/kbc,bq->qkc/dot_general | solution.py:91
  851.6 13.6 %fusion.94 = f32[128,32,512]{2,0,1:T(8,128)} fusion(f32[128,32,512]{2,0,1:T(8,128)S(1)} %fusion.68, f32[32,128,512]{2,0,1:T(8,128)S(1)} %bitcast.168), kind=kOutput, calls=%fused_computation.157 | convolution fusion | flops 3223552000 | bytes 25165824 | tf_op jit(solution)/shard_map/kbc,bq->qkc/dot_general | solution.py:88
  865.3 8.2 copy.96
  873.5 15.6 %fusion.97 = f32[128,32,512]{2,0,1:T(8,128)} fusion(f32[128,32,512]{2,0,1:T(8,128)} %fusion.66, f32[32,128,512]{2,0,1:T(8,128)S(1)} %bitcast.168), kind=kOutput, calls=%fused_computation.158 | convolution fusion | flops 3223552000 | bytes 25165824 | tf_op jit(solution)/shard_map/kbc,bq->qkc/dot_general | solution.py:91
  889.2 8.2 copy.99
  897.4 36.1 %fusion.65 = f32[4096,512]{1,0:T(8,128)} fusion(f32[128,32,512]{2,1,0:T(8,128)S(1)} %copy.99, f32[128,32,512]{2,1,0:T(8,128)S(1)} %copy.96, f32[512]{0:T(512)S(1)} %fusion.202, f32[4096]{0:T(1024)S(1)} %fusion.142, f32[]{:T(128)} %bitcast), kind=kLoop, calls=%fused_computation.125 | loop fusion | flops 12582912 | bytes 25184260 | tf_op jit(solution)/shard_map/sub | solution.py:175
  933.5 168.5 %reduce-scatter.2.cloned.1.call-done = f32[1024,512]{1,0:T(8,128)} async-done(((f32[4096,512]{1,0:T(8,128)}), f32[1024,512]{1,0:T(8,128)}) %reduce-scatter.2.cloned.1.call-update) | async-done | bytes 2097168 | tf_op jit(solution)/shard_map/reduce_scatter | solution.py:176
  (141 shorter events, 93.0 us)
Async XLA Ops:
  27.7 14.7 %all-to-all-start = ((f32[3,32,128]{2,0,1:T(4,128)}), f32[3,32,128]{2,0,1:T(4,128)S(1)}, u32[]{:S(2)}, u32[]{:S(2)}) async-start(f32[3,32,128]{2,0,1:T(4,128)} %copy.73), calls=%async_computation | async-start | bytes 131072 | tf_op jit(solution)/shard_map/all_to_all | solution.py:140
  35.1 1067.0 %reduce-scatter.2.cloned.1.call-start = ((), (), s32[]{:S(2)}) async-start(), calls=%async_computation.2 | async-start | bytes 10485760 | tf_op jit(solution)/shard_map/reduce_scatter | solution.py:176
  273.6 12.0 %collective-permute-start = (f32[2,7,4096]{2,1,0:T(8,128)S(1)}, f32[2,7,4096]{2,1,0:T(8,128)S(1)}, u32[]{:S(2)}, u32[]{:S(2)}) collective-permute-start(f32[2,7,4096]{2,1,0:T(8,128)S(1)} %slice.409), channel_id=1, source_target_pairs={{0,1},{1,2},{2,3},{3,4},{4,5},{5,6},{6,7},{7,0},{8,9},{9,10},{10,1... | collective-permute-start | bytes 688136 | tf_op jit(solution)/shard_map/ppermute | solution.py:25
  324.8 9.5 copy-start.3
  353.0 18.8 %copy-start.4 = (f32[512,32,128]{2,1,0:T(8,128)S(1)}, f32[512,32,128]{2,1,0:T(8,128)}, u32[]{:S(2)}) copy-start(f32[512,32,128]{2,1,0:T(8,128)} %get-tuple-element.234) | copy-start | bytes 25165828
  353.0 32.3 %slice-start.2 = ((s8[8388608]{0:T(1024)(128)(4,1)}), s8[4194304]{0:T(1024)(128)(4,1)S(1)}, s32[]{:S(2)}) async-start(s8[8388608]{0:T(1024)(128)(4,1)} %bitcast.169), calls=%async_computation.5 | async-start | bytes 8388608
  371.8 13.6 %slice-start.3 = ((s8[8388608]{0:T(1024)(128)(4,1)}), s8[4194304]{0:T(1024)(128)(4,1)S(1)}, s32[]{:S(2)}) async-start(s8[8388608]{0:T(1024)(128)(4,1)} %bitcast.169), calls=%async_computation.6 | async-start | bytes 8388608
  407.5 27.2 %copy-start = (f32[512,128,32]{0,2,1:T(8,128)}, f32[512,128,32]{0,2,1:T(8,128)S(1)}, u32[]{:S(2)}) copy-start(f32[512,128,32]{0,2,1:T(8,128)S(1)} %copy.79) | copy-start | bytes 25165828
  434.7 6.4 copy-start.1
  444.0 24.1 %collective-permute-start.1 = (f32[2,512,1,512]{3,1,0,2:T(8,128)}, f32[2,512,1,512]{3,1,0,2:T(8,128)}, u32[]{:S(2)}, u32[]{:S(2)}) collective-permute-start(f32[2,512,1,512]{3,1,0,2:T(8,128)} %bitcast.185), channel_id=1, source_target_pairs={{0,1},{1,0},{2,3},{3,2},{4,5},{5,4},{6,7},{7,6},{8,9},{9,8},{10,11... | collective-permute-start | bytes 6291464 | tf_op jit(solution)/shard_map/ppermute | solution.py:158
  447.3 131.5 %collective-permute-start.2 = (f32[2,512,1,512]{3,1,0,2:T(8,128)}, f32[2,512,1,512]{3,1,0,2:T(8,128)}, u32[]{:S(2)}, u32[]{:S(2)}) collective-permute-start(f32[2,512,1,512]{3,1,0,2:T(8,128)} %bitcast.183), channel_id=1, source_target_pairs={{0,2},{1,3},{2,0},{3,1},{4,6},{5,7},{6,4},{7,5},{8,10},{9,11},{10,... | collective-permute-start | bytes 6291464 | tf_op jit(solution)/shard_map/ppermute | solution.py:158
  450.7 171.2 %collective-permute-start.3 = (f32[2,512,1,512]{3,1,0,2:T(8,128)}, f32[2,512,1,512]{3,1,0,2:T(8,128)}, u32[]{:S(2)}, u32[]{:S(2)}) collective-permute-start(f32[2,512,1,512]{3,1,0,2:T(8,128)} %bitcast.182), channel_id=1, source_target_pairs={{0,3},{1,2},{2,1},{3,0},{4,7},{5,6},{6,5},{7,4},{8,11},{9,10},{10,... | collective-permute-start | bytes 6291464 | tf_op jit(solution)/shard_map/ppermute | solution.py:158
  454.6 170.4 %collective-permute-start.4 = (f32[2,512,1,512]{3,1,0,2:T(8,128)}, f32[2,512,1,512]{3,1,0,2:T(8,128)}, u32[]{:S(2)}, u32[]{:S(2)}) collective-permute-start(f32[2,512,1,512]{3,1,0,2:T(8,128)} %bitcast.181), channel_id=1, source_target_pairs={{0,4},{1,5},{2,6},{3,7},{4,0},{5,1},{6,2},{7,3},{8,12},{9,13},{10,... | collective-permute-start | bytes 6291464 | tf_op jit(solution)/shard_map/ppermute | solution.py:158
  464.7 263.9 %collective-permute-start.5 = (f32[2,512,1,512]{3,1,0,2:T(8,128)}, f32[2,512,1,512]{3,1,0,2:T(8,128)}, u32[]{:S(2)}, u32[]{:S(2)}) collective-permute-start(f32[2,512,1,512]{3,1,0,2:T(8,128)} %bitcast.184), channel_id=1, source_target_pairs={{0,5},{1,4},{2,7},{3,6},{4,1},{5,0},{6,3},{7,2},{8,13},{9,12},{10,... | collective-permute-start | bytes 6291464 | tf_op jit(solution)/shard_map/ppermute | solution.py:158
  468.1 263.5 %collective-permute-start.6 = (f32[2,512,1,512]{3,1,0,2:T(8,128)}, f32[2,512,1,512]{3,1,0,2:T(8,128)}, u32[]{:S(2)}, u32[]{:S(2)}) collective-permute-start(f32[2,512,1,512]{3,1,0,2:T(8,128)} %bitcast.186), channel_id=1, source_target_pairs={{0,6},{1,7},{2,4},{3,5},{4,2},{5,3},{6,0},{7,1},{8,14},{9,15},{10,... | collective-permute-start | bytes 6291464 | tf_op jit(solution)/shard_map/ppermute | solution.py:158
  578.8 156.0 %collective-permute-start.7 = (f32[2,512,1,512]{3,1,0,2:T(8,128)}, f32[2,512,1,512]{3,1,0,2:T(8,128)S(1)}, u32[]{:S(2)}, u32[]{:S(2)}) collective-permute-start(f32[2,512,1,512]{3,1,0,2:T(8,128)} %bitcast.187), channel_id=1, source_target_pairs={{0,7},{1,6},{2,5},{3,4},{4,3},{5,2},{6,1},{7,0},{8,15},{9,14},{10,... | collective-permute-start | bytes 6291464 | tf_op jit(solution)/shard_map/ppermute | solution.py:158
  757.1 26.4 %copy-start.5 = (f32[1,8,512,1,512]{4,2,0,1,3:T(8,128)}, f32[1,8,512,1,512]{4,2,0,1,3:T(8,128)S(1)}, u32[]{:S(2)}) copy-start(f32[1,8,512,1,512]{4,2,0,1,3:T(8,128)S(1)} %get-tuple-element.236) | copy-start | bytes 25165828
  821.2 17.0 %copy-start.2 = (f32[32,128,512]{2,0,1:T(8,128)S(1)}, f32[32,128,512]{2,0,1:T(8,128)}, u32[]{:S(2)}) copy-start(f32[32,128,512]{2,0,1:T(8,128)} %get-tuple-element.232) | copy-start | bytes 25165828
  821.2 30.4 %slice-start = ((s8[8388608]{0:T(1024)(128)(4,1)}), s8[4194304]{0:T(1024)(128)(4,1)S(1)}, s32[]{:S(2)}) async-start(s8[8388608]{0:T(1024)(128)(4,1)} %bitcast.167), calls=%async_computation.3 | async-start | bytes 8388608
  838.3 13.4 %slice-start.1 = ((s8[8388608]{0:T(1024)(128)(4,1)}), s8[4194304]{0:T(1024)(128)(4,1)S(1)}, s32[]{:S(2)}) async-start(s8[8388608]{0:T(1024)(128)(4,1)} %bitcast.167), calls=%async_computation.4 | async-start | bytes 8388608
Sparse Core Ops, SparseCore 0:
  933.7 168.3 reduce-scatter.1
